TPU v7x, 128 devices: a whole 4x4x4 slice. The times are simulated.
128 devices in a mesh: row: 8 (over y_hi, x), col: 16 (over z, y_lo, core).
Axes of the slice: x: 4, y: 4 (y_hi: 2, y_lo: 2; y = y_hi * 2 + y_lo), z: 4, core: 2. Of those that a mesh axis runs over, the one named last changes fastest.
Arguments:
- integrals: bfloat16 [2400, 2400, 256], P('row', 'col'), may hold values from -6 to 6
- occ_coef: bfloat16 [2400, 96], P('row'), may hold values from -0.125 to 0.125
- virt_coef: bfloat16 [2400, 2304], P('col'), may hold values from -0.125 to 0.125
- pair_index: int32 [256], replicated, may hold values from 0 to 255, each once
Outputs:
- transformed: bfloat16 [96, 2304, 256], P('row', 'col')
Inputs may be any that keep to these rules, and one draw needn't show every extreme that they name: pair_index holds each of 0 to 255 once.
All inputs are finite; a program needn't handle non-finite values.
Results may differ from a plain program's by a relative error of at most 0.0049.
Values may be sent and summed in bfloat16 or wider, within the bound.
A program may use at most 192 MiB of HBM per device.

v0:
```python
import jax
import jax.numpy as jnp
from jax import lax
from jax.sharding import PartitionSpec as P


def local(integrals, occ_coef, virt_coef, pair_index):
    half_rows = lax.psum_scatter(
        jnp.einsum("mi,mnp->inp", occ_coef, integrals, preferred_element_type=jnp.float32),
        "row",
        scatter_dimension=0,
        tiled=True,
    ).astype(jnp.bfloat16)
    virt_cols = lax.all_to_all(virt_coef, "col", split_axis=1, concat_axis=0, tiled=True)
    slab_local = jnp.einsum(
        "inp,na->iap",
        lax.all_gather(half_rows, "col", axis=1, tiled=True),
        virt_cols,
        preferred_element_type=jnp.float32,
    )
    slab_local = slab_local.astype(jnp.bfloat16)
    return jnp.take(slab_local, pair_index, axis=2)


def solution(mesh):
    return jax.shard_map(
        local,
        mesh=mesh,
        in_specs=(P("row", "col", None), P("row", None), P("col", None), P()),
        out_specs=P("row", "col", None),
        check_vma=False,
    )
```

profile of v0, /device:TPU:1, one launch (start us, length us, event | category | flops | bytes accessed | tf_op | source)
XLA Modules:
  0.0 363.8 jit_solution(18338669772870637867)
XLA Ops:
  6.5 0.0 copy-start
  6.5 0.0 reduce-scatter.2.cloned.1.call-start
  6.5 0.9 copy-done
  7.4 14.3 %fusion = f32[96,150,256]{2,0,1:T(8,128)} fusion(bf16[300,150,256]{2,1,0:T(8,128)(2,1)} %param.4, bf16[300,96]{0,1:T(8,128)(2,1)S(1)} %copy-done), kind=kOutput, calls=%fused_computation.1 | convolution fusion | flops 2211840000 | bytes 37843200 | tf_op jit(solution)/shard_map/mi,mnp->inp/dot_general | solution.py:9
  21.7 19.0 %copy.16 = f32[96,150,256]{2,1,0:T(8,128)} copy(f32[96,150,256]{2,0,1:T(8,128)} %fusion) | data formatting | bytes 29491200 | tf_op jit(solution)/shard_map/mi,mnp->inp/dot_general | solution.py:9
  40.7 0.0 reduce-scatter.2.cloned.1.call-update
  40.8 0.0 all-gather.2.cloned.1.call-start
  40.8 174.7 %reduce-scatter.2.cloned.1.call-done = f32[12,150,256]{2,1,0:T(8,128)} async-done(((f32[96,150,256]{2,1,0:T(8,128)}), f32[12,150,256]{2,1,0:T(8,128)}) %reduce-scatter.2.cloned.1.call-update) | async-done | bytes 1843216 | tf_op jit(solution)/shard_map/reduce_scatter | solution.py:8
  215.5 1.6 convert_element_type.9
  217.1 0.0 copy-start.2
  217.1 1.3 copy.17
  218.4 0.0 all-gather.2.cloned.1.call-update
  218.4 0.0 copy-done.2
  218.4 0.0 copy-start.3
  218.4 1.4 copy.23
  219.8 5.9 %all-to-all-start = ((bf16[150,16,144]{0,2,1:T(8,128)(2,1)}), bf16[150,16,144]{0,2,1:T(8,128)(2,1)S(1)}, u32[]{:S(2)}, u32[]{:S(2)}) async-start(bf16[150,16,144]{0,2,1:T(8,128)(2,1)} %bitcast.1), calls=%async_computation.1 | async-start | bytes 2359296 | tf_op jit(solution)/shard_map/all_to_all | solution.py:14
  225.7 0.0 copy-done.3
  225.8 29.2 %all-to-all-done = bf16[150,16,144]{0,2,1:T(8,128)(2,1)S(1)} async-done(((bf16[150,16,144]{0,2,1:T(8,128)(2,1)}), bf16[150,16,144]{0,2,1:T(8,128)(2,1)S(1)}, u32[]{:S(2)}, u32[]{:S(2)}) %all-to-all-start) | async-done | bytes 691232 | tf_op jit(solution)/shard_map/all_to_all | solution.py:14
  255.0 0.4 copy.19
  255.4 1.8 reshape.18
  257.1 78.2 %all-gather.2.cloned.1.call-done = bf16[12,2400,256]{2,0,1:T(8,128)(2,1)} async-done(((bf16[12,150,256]{2,0,1:T(8,128)(2,1)}), bf16[12,2400,256]{2,0,1:T(8,128)(2,1)}) %all-gather.2.cloned.1.call-update) | async-done | bytes 14745616 | tf_op jit(solution)/shard_map/all_gather | solution.py:17
  335.4 11.7 %fusion.7 = bf16[12,144,256]{2,1,0:T(8,128)(2,1)S(1)} fusion(bf16[2400,144,1]{0,1,2:T(8,128)(2,1)S(1)} %reshape.18, bf16[12,2400,256]{2,0,1:T(8,128)(2,1)} %all-gather.2.cloned.1.call-done), kind=kOutput, calls=%fused_computation.7 | convolution fusion | flops 2123808768 | bytes 16321536 | tf_op jit(solution)/shard_map/inp,na->iap/dot_general | solution.py:15
  347.1 3.1 copy.21
  350.2 2.1 gather_fusion
  352.2 0.0 copy-start.1
  352.2 2.2 select_bitcast_fusion
  354.4 2.5 copy.22
  356.9 0.0 copy-done.1
  (3 shorter events, 0.0 us)
Async XLA Ops:
  6.5 0.9 copy-start
  6.5 209.0 %reduce-scatter.2.cloned.1.call-start = ((), (), s32[]{:S(2)}) async-start(), calls=%async_computation.2 | async-start | bytes 16809984 | tf_op jit(solution)/shard_map/reduce_scatter | solution.py:8
  40.8 294.6 %all-gather.2.cloned.1.call-start = ((), (), s32[]{:S(2)}) async-start(), calls=%async_computation.3 | async-start | bytes 20889600 | tf_op jit(solution)/shard_map/all_gather | solution.py:17
  217.1 1.3 copy-start.2
  218.4 7.3 %copy-start.3 = (s32[256]{0:T(256)S(1)}, s32[256]{0:T(256)}, u32[]{:S(2)}) copy-start(s32[256]{0:T(256)} %param.7) | copy-start | bytes 3076
  219.8 35.2 %all-to-all-start = ((bf16[150,16,144]{0,2,1:T(8,128)(2,1)}), bf16[150,16,144]{0,2,1:T(8,128)(2,1)S(1)}, u32[]{:S(2)}, u32[]{:S(2)}) async-start(bf16[150,16,144]{0,2,1:T(8,128)(2,1)} %bitcast.1), calls=%async_computation.1 | async-start | bytes 2359296 | tf_op jit(solution)/shard_map/all_to_all | solution.py:14
  352.2 4.7 %copy-start.1 = (bf16[300,96]{0,1:T(8,128)(2,1)S(1)}, bf16[300,96]{0,1:T(8,128)(2,1)}, u32[]{:S(2)}) copy-start(bf16[300,96]{0,1:T(8,128)(2,1)} %param.5) | copy-start | bytes 172804
Sparse Core Ops, SparseCore 0:
  40.9 174.5 reduce-scatter.1
  218.5 116.8 all-gather.1
where the time goes:
time: 364 us
  waiting for transfers between devices  282 us (77%)
  local copies, waits for them, and re-layouts  32.4 us (9%)
  matrix products  26 us (7%)
  between operations  13.5 us (4%)
  starting transfers between devices  5.92 us (2%)
  other arithmetic  3.79 us (1%)
    reduce_scatter x1, waiting for transfers between devices, local(): lax.psum_scatter(jnp.einsum('mi,mnp->inp', occ_coef, integrals, preferred...  175 us
    all_gather x1, waiting for transfers between devices, local(): lax.all_gather(half_rows, 'col', axis=1, tiled=True)  78.2 us
    all_to_all x1, waiting for transfers between devices, local(): lax.all_to_all(virt_coef, 'col', split_axis=1, concat_axis=0, tiled=True)  29.2 us
    dot_general x1, local copies, waits for them, and re-layouts, local(): jnp.einsum('mi,mnp->inp', occ_coef, integrals, preferred_element_type=jnp...  19 us
    dot_general x1, matrix products, local(): jnp.einsum('mi,mnp->inp', occ_coef, integrals, preferred_element_type=jnp...  14.3 us
    dot_general x1, matrix products, local(): jnp.einsum('inp,na->iap', lax.all_gather(half_rows, 'col', axis=1, tiled=...  11.7 us
  transfers between devices with their start and end apart: 3, of which 3 were waited for; matrix products, arithmetic and copies ran while one was open for 1% of the time, Pallas kernels for 0%

commit v1 on v0

v1 whole, which is shorter than its diff:
```python
import functools

import jax
import jax.numpy as jnp
from jax import lax
from jax.experimental import pallas as pl
from jax.experimental.pallas import tpu as pltpu
from jax.sharding import PartitionSpec as P

MESH = pl.DeviceIdType.MESH
BF = jnp.bfloat16
F32 = jnp.float32

N_MU = 300
N_NU = 150
O_LOC = 12
A_LOC = 144
NP = 256
TILES = 19
CHUNKS = (4, 4, 4, 4, 3)
STARTS = tuple(sum(CHUNKS[:k]) for k in range(len(CHUNKS)))
BLK = O_LOC * 8
KROWS = N_MU * 8
NBUF = 3

(X1P, X1M, RAWP, RAWM, ACCP, ACCM, YH, AZP, AZM, AY, AC, BZP, BZM, BC, CZP, CZM, CCP, CCM, DC) = range(19)
NSEM = 19

ORDER = (
    ("M", 0), ("X", 0), ("M", 1), ("S", 0), ("X", 1), ("V", 0), ("Y", 0), ("M", 2), ("S", 1), ("X", 2),
    ("H", 0), ("Y", 1), ("B", 0), ("M", 3), ("S", 2), ("X", 3), ("C", 0), ("H", 1), ("B", 1), ("Y", 2),
    ("M", 4), ("S", 3), ("X", 4), ("D", 0), ("E", 0), ("C", 1), ("H", 2), ("B", 2), ("Y", 3), ("S", 4),
    ("D", 1), ("E", 1), ("C", 2), ("H", 3), ("B", 3), ("Y", 4), ("D", 2), ("E", 2), ("H", 4), ("B", 4), ("C", 3),
    ("D", 3), ("E", 3), ("C", 4), ("D", 4), ("E", 4),
)


def kernel(
    ints, occ_rep, virt, onehot, out,
    ibuf, kron, expand, part, r1p, r1m, r2p, r2m, ry, gath, vrecv, vrows, vt, acc,
    isem, vsend, vrecv_sem, send, recv,
):
    row = lax.axis_index("row")
    col = lax.axis_index("col")
    yh, x = row // 4, row % 4
    z, yl, core = col // 4, (col // 2) % 2, col % 2
    xp, xm = (x + 1) % 4, (x + 3) % 4
    x2 = (x + 2) % 4
    zp, zm, z2 = (z + 1) % 4, (z + 3) % 4, (z + 2) % 4

    def rowid(xx, yy):
        return {"row": yy * 4 + xx}

    def colid(zz, ll, cc):
        return {"col": zz * 4 + ll * 2 + cc}

    d_xp, d_xm, d_yh = rowid(xp, yh), rowid(xm, yh), rowid(x, 1 - yh)
    d_zp, d_zm = colid(zp, yl, core), colid(zm, yl, core)
    d_yl, d_co = colid(z, 1 - yl, core), colid(z, yl, 1 - core)

    def slot(zz, ll, cc):
        return cc * 8 + zz * 2 + ll

    me = slot(z, yl, core)

    barrier = pltpu.get_barrier_semaphore()
    for d in (d_xp, d_xm, d_yh):
        pl.semaphore_signal(barrier, inc=1, device_id=d, device_id_type=MESH)

    @pl.loop(1, 16)
    def _(k):
        pl.semaphore_signal(barrier, inc=1, device_id={"col": (col + k) % 16}, device_id_type=MESH)

    def icopy(t, s):
        return pltpu.make_async_copy(ints.at[:, pl.ds(pl.multiple_of(t * 8, 8), 8), :], ibuf.at[s], isem.at[s])

    def icopy_last(s):
        return pltpu.make_async_copy(
            ints.at[:, pl.ds(8 * (TILES - 1), 6), :], ibuf.at[s, :, pl.ds(0, 6), :], isem.at[s]
        )

    for t in range(NBUF):
        icopy(t, t).start()

    expand[...] = jnp.where(
        lax.broadcasted_iota(jnp.int32, (N_MU, KROWS), 0) == lax.broadcasted_iota(jnp.int32, (N_MU, KROWS), 1) // 8,
        1.0, 0.0,
    ).astype(BF)

    @pl.loop(0, 8)
    def _(b):
        rows = pl.ds(pl.multiple_of(b * BLK, BLK), BLK)
        wide = jnp.dot(occ_rep[rows, :], expand[...], preferred_element_type=F32)
        same = (
            lax.broadcasted_iota(jnp.int32, (BLK, KROWS), 0) % 8 == lax.broadcasted_iota(jnp.int32, (BLK, KROWS), 1) % 8
        )
        kron[rows, :] = jnp.where(same, wide, 0.0).astype(BF)

    pl.semaphore_wait(barrier, 18)

    sent = []

    def remote(src, dst, c, k, dev):
        cp = pltpu.make_async_remote_copy(
            src_ref=src, dst_ref=dst, send_sem=send.at[c * NSEM + k], recv_sem=recv.at[c * NSEM + k],
            device_id=dev, device_id_type=MESH,
        )
        return cp

    cps = {}

    def go(c, k, src, dst, dev):
        cp = remote(src, dst, c, k, dev)
        cp.start()
        cps[c, k] = cp
        sent.append(cp)

    def vcopy(k):
        to = (col + k) % 16
        to_slot = slot(to // 4, (to // 2) % 2, to % 2)
        return pltpu.make_async_remote_copy(
            src_ref=virt.at[to_slot], dst_ref=vrecv.at[me], send_sem=vsend.at[k], recv_sem=vrecv_sem.at[k],
            device_id={"col": to}, device_id_type=MESH,
        )

    def vlocal():
        return pltpu.make_async_copy(virt.at[me], vrecv.at[me], vsend.at[0])

    vlocal().start()

    @pl.loop(1, 16)
    def _(k):
        vcopy(k).start()

    def tiles(c):
        return pl.ds(STARTS[c], CHUNKS[c])

    def blk(xx, yy):
        return pl.ds(pl.multiple_of(xx * (2 * BLK) + yy * BLK, BLK), BLK)

    def task_m(c):
        @pl.loop(STARTS[c], STARTS[c] + CHUNKS[c])
        def _(t):
            s = t % NBUF

            @pl.when(t < TILES - 1)
            def _():
                icopy(t, s).wait()

            @pl.when(t == TILES - 1)
            def _():
                icopy_last(s).wait()

            rhs = ibuf[s].reshape(KROWS, NP)
            part[t] = jnp.dot(kron[...], rhs, preferred_element_type=F32).astype(BF)

            @pl.when(t + NBUF < TILES - 1)
            def _():
                icopy(t + NBUF, s).start()

            @pl.when(t + NBUF == TILES - 1)
            def _():
                icopy_last(s).start()

    def task_x(c):
        ts = tiles(c)
        go(c, X1P, part.at[ts, blk(x2, 0)], r1p.at[ts], d_xp)
        go(c, X1M, part.at[ts, blk(x2, 1)], r1m.at[ts], d_xm)
        go(c, RAWP, part.at[ts, blk(xp, 1)], r2p.at[ts, pl.ds(BLK, BLK)], d_xp)
        go(c, RAWM, part.at[ts, blk(xm, 0)], r2m.at[ts, pl.ds(0, BLK)], d_xm)

    def each_tile(c, body):
        pl.loop(STARTS[c], STARTS[c] + CHUNKS[c])(body)

    def task_s(c):
        ts = tiles(c)
        cps[c, X1P].wait_recv()

        @functools.partial(each_tile, c)
        def _(t):
            b = blk(xp, 0)
            part[t, b, :] = (part[t, b, :].astype(F32) + r1p[t].astype(F32)).astype(BF)

        go(c, ACCP, part.at[ts, blk(xp, 0)], r2p.at[ts, pl.ds(0, BLK)], d_xp)
        cps[c, X1M].wait_recv()

        @functools.partial(each_tile, c)
        def _(t):
            b = blk(xm, 1)
            part[t, b, :] = (part[t, b, :].astype(F32) + r1m[t].astype(F32)).astype(BF)

        go(c, ACCM, part.at[ts, blk(xm, 1)], r2m.at[ts, pl.ds(BLK, BLK)], d_xm)

    def xsum(t, yy):
        side = pl.ds(pl.multiple_of(yy * BLK, BLK), BLK)
        return part[t, blk(x, yy), :].astype(F32) + r2p[t, side, :].astype(F32) + r2m[t, side, :].astype(F32)

    def task_y(c):
        ts = tiles(c)
        for k in (RAWP, RAWM, ACCP, ACCM):
            cps[c, k].wait_recv()

        @functools.partial(each_tile, c)
        def _(t):
            part[t, blk(x, 1 - yh), :] = xsum(t, 1 - yh).astype(BF)

        go(c, YH, part.at[ts, blk(x, 1 - yh)], ry.at[ts], d_yh)

    def grows(c, s, count=1):
        n = 8 * CHUNKS[c]
        return pl.ds(pl.multiple_of(128 * STARTS[c] + s * n, 8), count * n)

    def whole(c, s, count=1):
        return gath.at[:, grows(c, s, count), :]

    def half(c, s, lo):
        return gath.at[pl.ds(lo, O_LOC // 2), grows(c, s, 2), :]

    def task_h(c):
        cps[c, YH].wait_recv()
        base = 128 * STARTS[c] + me * (8 * CHUNKS[c])

        @functools.partial(each_tile, c)
        def _(t):
            h = (xsum(t, yh) + ry[t].astype(F32)).astype(BF)
            h = jnp.dot(h, onehot[...], preferred_element_type=F32).astype(BF)
            dst = pl.ds(pl.multiple_of(base + (t - STARTS[c]) * 8, 8), 8)
            gath[:, dst, :] = h.reshape(O_LOC, 8, NP)

        g = whole(c, me)
        go(c, AY, g, g, d_yl)
        go(c, AZP, g, g, d_zp)
        go(c, AZM, g, g, d_zm)
        go(c, AC, g, g, d_co)

    def task_b(c):
        cps[c, AY].wait_recv()
        g = whole(c, slot(z, 1 - yl, core))
        go(c, BZP, g, g, d_zp)
        go(c, BZM, g, g, d_zm)
        go(c, BC, g, g, d_co)

    def task_c(c):
        cps[c, AZP].wait_recv()
        cps[c, BZP].wait_recv()
        s = slot(zm, 0, core)
        g = half(c, s, 0)
        go(c, CZP, g, g, d_zp)
        g = whole(c, s, 2)
        go(c, CCP, g, g, d_co)
        cps[c, AZM].wait_recv()
        cps[c, BZM].wait_recv()
        s = slot(zp, 0, core)
        g = half(c, s, O_LOC // 2)
        go(c, CZM, g, g, d_zm)
        g = whole(c, s, 2)
        go(c, CCM, g, g, d_co)

    def task_d(c):
        cps[c, CZP].wait_recv()
        cps[c, CZM].wait_recv()
        g = whole(c, slot(z2, 0, core), 2)
        go(c, DC, g, g, d_co)

    def task_v(_):
        vlocal().wait()

        @pl.loop(1, 16)
        def _(k):
            vcopy(k).wait()

        for c in range(len(CHUNKS)):
            n = 8 * CHUNKS[c]

            @pl.loop(0, 16)
            def _(s):
                dst = pl.ds(pl.multiple_of(128 * STARTS[c] + s * n, 8), n)
                vrows[dst, :] = vrecv[s, pl.ds(8 * STARTS[c], n), :]

        @pl.loop(0, TILES)
        def _(t):
            o = pl.multiple_of(t * 128, 128)
            vt[:, pl.ds(o, 128)] = vrows[pl.ds(o, 128), :].astype(F32).T[:A_LOC].astype(BF)

    def task_e(c):
        for k in (AC, BC, CCP, CCM, DC):
            cps[c, k].wait_recv()
        ks = pl.ds(128 * STARTS[c], 128 * CHUNKS[c])
        lhs = vt[:, ks]
        last = c == len(CHUNKS) - 1

        @pl.loop(0, O_LOC)
        def _(i):
            d = jnp.dot(lhs, gath[i, ks, :], preferred_element_type=F32)
            if c > 0:
                d = d + acc[i]
            if last:
                out[i] = d.astype(BF)
            else:
                acc[i] = d

    tasks = {"M": task_m, "X": task_x, "S": task_s, "Y": task_y, "H": task_h, "B": task_b, "C": task_c,
             "D": task_d, "E": task_e, "V": task_v}
    for name, c in ORDER:
        tasks[name](c)
    for cp in sent:
        cp.wait_send()


def local(integrals, occ_coef, virt_coef, pair_index):
    occ = occ_coef.T.reshape(2, 4, O_LOC, N_MU).transpose(1, 0, 2, 3).reshape(8 * O_LOC, N_MU)
    occ_rep = jnp.repeat(occ, 8, axis=0)
    virt = virt_coef.reshape(N_NU, 4, 2, 2, A_LOC).transpose(3, 1, 2, 0, 4).reshape(16, N_NU, A_LOC)
    virt = jnp.pad(virt, ((0, 0), (0, 8 * TILES - N_NU), (0, NP - A_LOC)))
    onehot = (jnp.arange(NP, dtype=jnp.int32)[:, None] == pair_index[None, :]).astype(BF)
    nsem = NSEM * len(CHUNKS)
    vm = pl.BlockSpec(memory_space=pltpu.VMEM)
    hbm = pl.BlockSpec(memory_space=pl.ANY)
    return pl.pallas_call(
        kernel,
        out_shape=jax.ShapeDtypeStruct((O_LOC, A_LOC, NP), BF),
        in_specs=[hbm, vm, hbm, vm],
        out_specs=vm,
        scratch_shapes=[
            pltpu.VMEM((NBUF, N_MU, 8, NP), BF),
            pltpu.VMEM((8 * BLK, KROWS), BF),
            pltpu.VMEM((N_MU, KROWS), BF),
            pltpu.VMEM((TILES, 8 * BLK, NP), BF),
            pltpu.VMEM((TILES, BLK, NP), BF),
            pltpu.VMEM((TILES, BLK, NP), BF),
            pltpu.VMEM((TILES, 2 * BLK, NP), BF),
            pltpu.VMEM((TILES, 2 * BLK, NP), BF),
            pltpu.VMEM((TILES, BLK, NP), BF),
            pltpu.VMEM((O_LOC, TILES * 128, NP), BF),
            pltpu.VMEM((16, 8 * TILES, NP), BF),
            pltpu.VMEM((TILES * 128, NP), BF),
            pltpu.VMEM((A_LOC, TILES * 128), BF),
            pltpu.VMEM((O_LOC, A_LOC, NP), F32),
            pltpu.SemaphoreType.DMA((NBUF,)),
            pltpu.SemaphoreType.DMA((16,)),
            pltpu.SemaphoreType.DMA((16,)),
            pltpu.SemaphoreType.DMA((nsem,)),
            pltpu.SemaphoreType.DMA((nsem,)),
        ],
        compiler_params=pltpu.CompilerParams(
            collective_id=0, has_side_effects=True, vmem_limit_bytes=60 * 2**20
        ),
    )(integrals, occ_rep, virt, onehot)


def solution(mesh):
    return jax.shard_map(
        local,
        mesh=mesh,
        in_specs=(P("row", "col", None), P("row", None), P("col", None), P()),
        out_specs=P("row", "col", None),
        check_vma=False,
    )
```

time: 364 us -> 131 us (0.36)
  waiting for transfers between devices: 282 us -> 0 us
  Pallas kernels: 0 us -> 121 us
  matrix products: 26 us -> 0 us
  local copies, waits for them, and re-layouts: 32.4 us -> 9.86 us
  between operations: 13.5 us -> 0.05 us
  starting transfers between devices: 5.92 us -> 0 us
    reduce_scatter x1 -> x0, waiting for transfers between devices: 175 us -> none  [local(): lax.psum_scatter(jnp.einsum('mi,mnp->inp', occ_coef, integrals, preferred...]
    pallas_call x0 -> x1, Pallas kernels: none -> 121 us  [local(): pl.pallas_call(kernel, out_shape=jax.ShapeDtypeStruct((O_LOC, A_LOC, NP),...]
    all_gather x1 -> x0, waiting for transfers between devices: 78.2 us -> none  [local(): lax.all_gather(half_rows, 'col', axis=1, tiled=True)]
    all_to_all x1 -> x0, waiting for transfers between devices: 29.2 us -> none  [local(): lax.all_to_all(virt_coef, 'col', split_axis=1, concat_axis=0, tiled=True)]
    dot_general x2 -> x0, matrix products: 26 us -> none  [the longest x1 14.3 us: local(): jnp.einsum('mi,mnp->inp', occ_coef, integrals, preferred_element_type=jnp...]
    dot_general x1 -> x0, local copies, waits for them, and re-layouts: 19 us -> none  [local(): jnp.einsum('mi,mnp->inp', occ_coef, integrals, preferred_element_type=jnp...]
    reshape x0 -> x4, local copies, waits for them, and re-layouts: none -> 6.05 us  [the longest x1 5.1 us: local(): virt_coef.reshape(N_NU, 4, 2, 2, A_LOC).transpose(3, 1, 2, 0, 4)]
    all_to_all x1 -> x0, starting transfers between devices: 5.88 us -> none  [local(): lax.all_to_all(virt_coef, 'col', split_axis=1, concat_axis=0, tiled=True)]
  transfers between devices with their start and end apart: 3 -> 0, of which waited for: 3 -> 0; matrix products, arithmetic and copies ran while one was open for 1% -> 0% of each run, Pallas kernels for 0% -> 0%
where the time goes in v1:
time: 131 us
  Pallas kernels  121 us (92%)
  local copies, waits for them, and re-layouts  9.86 us (8%)
    pallas_call x1, Pallas kernels, local(): pl.pallas_call(kernel, out_shape=jax.ShapeDtypeStruct((O_LOC, A_LOC, NP),...  121 us
    reshape x1, local copies, waits for them, and re-layouts, local(): virt_coef.reshape(N_NU, 4, 2, 2, A_LOC).transpose(3, 1, 2, 0, 4)  5.1 us

profile of v1, /device:TPU:1, one launch (start us, length us, event | category | flops | bytes accessed | tf_op | source)
XLA Modules:
  0.0 131.1 jit_solution(6917247938390784291)
XLA Ops:
  0.0 5.1 %reshape.19 = bf16[150,4,2,2,144]{4,3,2,1,0:T(2,128)(2,1)S(1)} reshape(bf16[150,2304]{1,0:T(8,128)(2,1)} %param.6) | data formatting | bytes 1382400 | tf_op jit(solution)/shard_map/reshape | solution.py:313
  5.1 0.4 copy.7
  5.5 0.0 copy-start
  5.5 0.0 copy-start.1
  5.5 1.2 pad.4.virt
  6.8 0.0 copy-done
  6.9 0.9 broadcast_bitcast_fusion.occ_rep
  7.8 0.0 copy-done.1
  7.8 0.7 fusion.onehot
  8.4 120.5 %shard_map.46 = bf16[12,144,256]{2,1,0:T(8,128)(2,1)} custom-call(bf16[300,150,256]{2,1,0:T(8,128)(2,1)} %ints.1, bf16[768,300]{1,0:T(8,128)(2,1)} %broadcast_bitcast_fusion.occ_rep, bf16[16,152,256]{2,1,0:T(8,128)(2,1)} %pad.4.virt, bf16[256,256]{1,0:T(8,128)(2,1)} %fusion.onehot), custom_call_target="tpu_custom_call" | custom-call | tf_op jit(solution)/shard_map/pallas_call | solution.py:319
  129.0 2.1 %copy.9 = bf16[12,144,256]{2,1,0:T(8,128)(2,1)} copy(bf16[12,144,256]{2,1,0:T(8,128)(2,1)} %shard_map.46) | data formatting | bytes 1769472
  (3 shorter events, 0.1 us)
Async XLA Ops:
  5.5 1.3 copy-start
  5.5 2.2 %copy-start.1 = (s32[256]{0:T(256)S(1)}, s32[256]{0:T(256)}, u32[]{:S(2)}) copy-start(s32[256]{0:T(256)} %param.7) | copy-start | bytes 3076

commit v2 on v1

--- a/solution.py
+++ b/solution.py
@@ -17,7 +17,7 @@
 A_LOC = 144
 NP = 256
 TILES = 19
-CHUNKS = (4, 4, 4, 4, 3)
+CHUNKS = (2, 2, 3, 2, 3, 2, 2, 3)
 STARTS = tuple(sum(CHUNKS[:k]) for k in range(len(CHUNKS)))
 BLK = O_LOC * 8
 KROWS = N_MU * 8
@@ -27,18 +27,23 @@
 NSEM = 19
 
 ORDER = (
-    ("M", 0), ("X", 0), ("M", 1), ("S", 0), ("X", 1), ("V", 0), ("Y", 0), ("M", 2), ("S", 1), ("X", 2),
-    ("H", 0), ("Y", 1), ("B", 0), ("M", 3), ("S", 2), ("X", 3), ("C", 0), ("H", 1), ("B", 1), ("Y", 2),
-    ("M", 4), ("S", 3), ("X", 4), ("D", 0), ("E", 0), ("C", 1), ("H", 2), ("B", 2), ("Y", 3), ("S", 4),
-    ("D", 1), ("E", 1), ("C", 2), ("H", 3), ("B", 3), ("Y", 4), ("D", 2), ("E", 2), ("H", 4), ("B", 4), ("C", 3),
-    ("D", 3), ("E", 3), ("C", 4), ("D", 4), ("E", 4),
+    ("VS", 0), ("VP", 0), ("M", 0, 0, 2), ("X", 0), ("M", 1, 0, 2), ("X", 1), ("SM", 0), ("SP", 0), ("M", 2, 0, 2),
+    ("SM", 1), ("SP", 1), ("M", 2, 2, 1), ("M", 3, 0, 2), ("X", 2), ("Y", 0), ("Y", 1), ("M", 4, 0, 2), ("X", 3),
+    ("SM", 2), ("SP", 2), ("H", 0), ("H", 1), ("SM", 3), ("SP", 3), ("B", 0), ("M", 4, 2, 1), ("B", 1),
+    ("M", 5, 0, 2), ("X", 4), ("Y", 2), ("CM", 0), ("CP", 0), ("CM", 1), ("CP", 1), ("Y", 3), ("M", 6, 0, 2),
+    ("X", 5), ("D", 0), ("SM", 4), ("SP", 4), ("H", 2), ("D", 1), ("H", 3), ("SM", 5), ("SP", 5), ("M", 7, 0, 2),
+    ("B", 2), ("M", 7, 2, 1), ("X", 6), ("B", 3), ("Y", 4), ("Y", 5), ("X", 7), ("CM", 2), ("CP", 2), ("SM", 6),
+    ("SP", 6), ("CM", 3), ("CP", 3), ("H", 4), ("D", 2), ("H", 5), ("SM", 7), ("SP", 7), ("D", 3), ("VT", 0),
+    ("B", 4), ("Y", 6), ("B", 5), ("E", 0), ("Y", 7), ("CM", 4), ("CP", 4), ("H", 6), ("CM", 5), ("CP", 5), ("E", 1),
+    ("D", 4), ("H", 7), ("B", 6), ("E", 2), ("D", 5), ("E", 3), ("B", 7), ("E", 4), ("CM", 6), ("CP", 6), ("E", 5),
+    ("CM", 7), ("CP", 7), ("D", 6), ("E", 6), ("D", 7), ("E", 7),
 )
 
 
 def kernel(
-    ints, occ_rep, virt, onehot, out,
-    ibuf, kron, expand, part, r1p, r1m, r2p, r2m, ry, gath, vrecv, vrows, vt, acc,
-    isem, vsend, vrecv_sem, send, recv,
+    ints, occ_t, virt, index, out,
+    ibuf, kron, expand, occ_rep, onehot, part, r1p, r1m, r2p, r2m, ry, gath, vraw, vblk, vrecv, vrows, vt, acc,
+    isem, vload, vsend, vrecv_sem, send, recv,
 ):
     row = lax.axis_index("row")
     col = lax.axis_index("col")
@@ -82,19 +87,28 @@
     for t in range(NBUF):
         icopy(t, t).start()
 
-    expand[...] = jnp.where(
-        lax.broadcasted_iota(jnp.int32, (N_MU, KROWS), 0) == lax.broadcasted_iota(jnp.int32, (N_MU, KROWS), 1) // 8,
-        1.0, 0.0,
-    ).astype(BF)
-
-    @pl.loop(0, 8)
+    def vfetch():
+        return pltpu.make_async_copy(virt, vraw, vload)
+
+    vfetch().start()
+
+    def iota(shape, axis):
+        return lax.broadcasted_iota(jnp.int32, shape, axis)
+
+    for b in range(8):
+        first = ((b % 2) * 4 + b // 2) * O_LOC
+        pick = jnp.where(iota((BLK, BLK), 1) == first + (iota((BLK, BLK), 0) >> 3), 1.0, 0.0).astype(BF)
+        occ_rep[b * BLK : (b + 1) * BLK, :] = jnp.dot(pick, occ_t[...], preferred_element_type=F32).astype(BF)
+    expand[...] = jnp.where(iota((N_MU, KROWS), 0) == (iota((N_MU, KROWS), 1) >> 3), 1.0, 0.0).astype(BF)
+
+    @pl.loop(0, 4)
     def _(b):
-        rows = pl.ds(pl.multiple_of(b * BLK, BLK), BLK)
+        rows = pl.ds(pl.multiple_of(b * (2 * BLK), 2 * BLK), 2 * BLK)
         wide = jnp.dot(occ_rep[rows, :], expand[...], preferred_element_type=F32)
-        same = (
-            lax.broadcasted_iota(jnp.int32, (BLK, KROWS), 0) % 8 == lax.broadcasted_iota(jnp.int32, (BLK, KROWS), 1) % 8
-        )
+        same = (iota((2 * BLK, KROWS), 0) & 7) == (iota((2 * BLK, KROWS), 1) & 7)
         kron[rows, :] = jnp.where(same, wide, 0.0).astype(BF)
+
+    onehot[...] = jnp.where(iota((NP, NP), 0) == index[...], 1.0, 0.0).astype(BF)
 
     pl.semaphore_wait(barrier, 18)
 
@@ -119,18 +133,26 @@
         to = (col + k) % 16
         to_slot = slot(to // 4, (to // 2) % 2, to % 2)
         return pltpu.make_async_remote_copy(
-            src_ref=virt.at[to_slot], dst_ref=vrecv.at[me], send_sem=vsend.at[k], recv_sem=vrecv_sem.at[k],
+            src_ref=vblk.at[to_slot], dst_ref=vrecv.at[me], send_sem=vsend.at[k], recv_sem=vrecv_sem.at[k],
             device_id={"col": to}, device_id_type=MESH,
         )
 
     def vlocal():
-        return pltpu.make_async_copy(virt.at[me], vrecv.at[me], vsend.at[0])
-
-    vlocal().start()
-
-    @pl.loop(1, 16)
-    def _(k):
-        vcopy(k).start()
+        return pltpu.make_async_copy(vblk.at[me], vrecv.at[me], vsend.at[0])
+
+    def task_vs(_):
+        vfetch().wait()
+        for k in range(16):
+            s = slot(k // 4, (k // 2) % 2, k % 2)
+            vblk[s, N_NU - 6 : 8 * TILES, :] = jnp.zeros((8, NP), BF)
+            vblk[s, 0:N_NU, 0:A_LOC] = vraw[:, k * A_LOC : (k + 1) * A_LOC]
+
+    def task_vp(_):
+        vlocal().start()
+
+        @pl.loop(1, 16)
+        def _(k):
+            vcopy(k).start()
 
     def tiles(c):
         return pl.ds(STARTS[c], CHUNKS[c])
@@ -138,8 +160,8 @@
     def blk(xx, yy):
         return pl.ds(pl.multiple_of(xx * (2 * BLK) + yy * BLK, BLK), BLK)
 
-    def task_m(c):
-        @pl.loop(STARTS[c], STARTS[c] + CHUNKS[c])
+    def task_m(c, first, count):
+        @pl.loop(STARTS[c] + first, STARTS[c] + first + count)
         def _(t):
             s = t % NBUF
 
@@ -172,7 +194,7 @@
     def each_tile(c, body):
         pl.loop(STARTS[c], STARTS[c] + CHUNKS[c])(body)
 
-    def task_s(c):
+    def task_sp(c):
         ts = tiles(c)
         cps[c, X1P].wait_recv()
 
@@ -182,6 +204,9 @@
             part[t, b, :] = (part[t, b, :].astype(F32) + r1p[t].astype(F32)).astype(BF)
 
         go(c, ACCP, part.at[ts, blk(xp, 0)], r2p.at[ts, pl.ds(0, BLK)], d_xp)
+
+    def task_sm(c):
+        ts = tiles(c)
         cps[c, X1M].wait_recv()
 
         @functools.partial(each_tile, c)
@@ -240,7 +265,7 @@
         go(c, BZM, g, g, d_zm)
         go(c, BC, g, g, d_co)
 
-    def task_c(c):
+    def task_cp(c):
         cps[c, AZP].wait_recv()
         cps[c, BZP].wait_recv()
         s = slot(zm, 0, core)
@@ -248,6 +273,8 @@
         go(c, CZP, g, g, d_zp)
         g = whole(c, s, 2)
         go(c, CCP, g, g, d_co)
+
+    def task_cm(c):
         cps[c, AZM].wait_recv()
         cps[c, BZM].wait_recv()
         s = slot(zp, 0, core)
@@ -262,7 +289,7 @@
         g = whole(c, slot(z2, 0, core), 2)
         go(c, DC, g, g, d_co)
 
-    def task_v(_):
+    def task_vt(_):
         vlocal().wait()
 
         @pl.loop(1, 16)
@@ -299,20 +326,15 @@
             else:
                 acc[i] = d
 
-    tasks = {"M": task_m, "X": task_x, "S": task_s, "Y": task_y, "H": task_h, "B": task_b, "C": task_c,
-             "D": task_d, "E": task_e, "V": task_v}
-    for name, c in ORDER:
-        tasks[name](c)
+    tasks = {"M": task_m, "X": task_x, "SP": task_sp, "SM": task_sm, "Y": task_y, "H": task_h, "B": task_b,
+             "CP": task_cp, "CM": task_cm, "D": task_d, "E": task_e, "VS": task_vs, "VP": task_vp, "VT": task_vt}
+    for name, *where in ORDER:
+        tasks[name](*where)
     for cp in sent:
         cp.wait_send()
 
 
 def local(integrals, occ_coef, virt_coef, pair_index):
-    occ = occ_coef.T.reshape(2, 4, O_LOC, N_MU).transpose(1, 0, 2, 3).reshape(8 * O_LOC, N_MU)
-    occ_rep = jnp.repeat(occ, 8, axis=0)
-    virt = virt_coef.reshape(N_NU, 4, 2, 2, A_LOC).transpose(3, 1, 2, 0, 4).reshape(16, N_NU, A_LOC)
-    virt = jnp.pad(virt, ((0, 0), (0, 8 * TILES - N_NU), (0, NP - A_LOC)))
-    onehot = (jnp.arange(NP, dtype=jnp.int32)[:, None] == pair_index[None, :]).astype(BF)
     nsem = NSEM * len(CHUNKS)
     vm = pl.BlockSpec(memory_space=pltpu.VMEM)
     hbm = pl.BlockSpec(memory_space=pl.ANY)
@@ -325,6 +347,8 @@
             pltpu.VMEM((NBUF, N_MU, 8, NP), BF),
             pltpu.VMEM((8 * BLK, KROWS), BF),
             pltpu.VMEM((N_MU, KROWS), BF),
+            pltpu.VMEM((8 * BLK, N_MU), BF),
+            pltpu.VMEM((NP, NP), BF),
             pltpu.VMEM((TILES, 8 * BLK, NP), BF),
             pltpu.VMEM((TILES, BLK, NP), BF),
             pltpu.VMEM((TILES, BLK, NP), BF),
@@ -332,11 +356,14 @@
             pltpu.VMEM((TILES, 2 * BLK, NP), BF),
             pltpu.VMEM((TILES, BLK, NP), BF),
             pltpu.VMEM((O_LOC, TILES * 128, NP), BF),
+            pltpu.VMEM((N_NU, 16 * A_LOC), BF),
+            pltpu.VMEM((16, 8 * TILES, NP), BF),
             pltpu.VMEM((16, 8 * TILES, NP), BF),
             pltpu.VMEM((TILES * 128, NP), BF),
             pltpu.VMEM((A_LOC, TILES * 128), BF),
             pltpu.VMEM((O_LOC, A_LOC, NP), F32),
             pltpu.SemaphoreType.DMA((NBUF,)),
+            pltpu.SemaphoreType.DMA,
             pltpu.SemaphoreType.DMA((16,)),
             pltpu.SemaphoreType.DMA((16,)),
             pltpu.SemaphoreType.DMA((nsem,)),
@@ -345,7 +372,7 @@
         compiler_params=pltpu.CompilerParams(
             collective_id=0, has_side_effects=True, vmem_limit_bytes=60 * 2**20
         ),
-    )(integrals, occ_rep, virt, onehot)
+    )(integrals, occ_coef.T, virt_coef, pair_index[None, :])
 
 
 def solution(mesh):

time: 131 us -> 109 us (0.83)
  Pallas kernels: 121 us -> 107 us
  local copies, waits for them, and re-layouts: 9.86 us -> 2.14 us
    pallas_call x1, Pallas kernels: 121 us -> 107 us  [local(): pl.pallas_call(kernel, out_shape=jax.ShapeDtypeStruct((O_LOC, A_LOC, NP),...]
    reshape x4 -> x0, local copies, waits for them, and re-layouts: 6.05 us -> none  [the longest x1 5.1 us: local(): virt_coef.reshape(N_NU, 4, 2, 2, A_LOC).transpose(3, 1, 2, 0, 4)]
where the time goes in v2:
time: 109 us
  Pallas kernels  107 us (98%)
  local copies, waits for them, and re-layouts  2.14 us (2%)
    pallas_call x1, Pallas kernels, local(): pl.pallas_call(kernel, out_shape=jax.ShapeDtypeStruct((O_LOC, A_LOC, NP),...  107 us

profile of v2, /device:TPU:1, one launch (start us, length us, event | category | flops | bytes accessed | tf_op | source)
XLA Modules:
  0.0 109.2 jit_solution(16802219603815820869)
XLA Ops:
  0.0 107.1 %shard_map.46 = bf16[12,144,256]{2,1,0:T(8,128)(2,1)} custom-call(bf16[300,150,256]{2,1,0:T(8,128)(2,1)} %ints.1, bf16[96,300]{1,0:T(8,128)(2,1)} %bitcast.2, bf16[150,2304]{1,0:T(8,128)(2,1)} %virt.1, s32[1,256]{1,0:T(1,128)} %bitcast.3), custom_call_target="tpu_custom_call" | custom-call | tf_op jit(solution)/shard_map/pallas_call | solution.py:341
  107.1 2.1 %copy.6 = bf16[12,144,256]{2,1,0:T(8,128)(2,1)} copy(bf16[12,144,256]{2,1,0:T(8,128)(2,1)} %shard_map.46) | data formatting | bytes 1769472

commit v3 on v2

--- a/solution.py
+++ b/solution.py
@@ -17,32 +17,34 @@
 A_LOC = 144
 NP = 256
 TILES = 19
-CHUNKS = (2, 2, 3, 2, 3, 2, 2, 3)
+CHUNKS = (2, 2, 3, 2, 2, 3, 3, 2)
+Z_FIRST = (6,)
 STARTS = tuple(sum(CHUNKS[:k]) for k in range(len(CHUNKS)))
 BLK = O_LOC * 8
 KROWS = N_MU * 8
 NBUF = 3
 
-(X1P, X1M, RAWP, RAWM, ACCP, ACCM, YH, AZP, AZM, AY, AC, BZP, BZM, BC, CZP, CZM, CCP, CCM, DC) = range(19)
-NSEM = 19
+(X1P, X1M, RAWP, RAWM, ACCP, ACCM, YH, AZP, AZM, AY, AC, BZP, BZM, BC, CZP, CZM, CCP, CCM, DC,
+ BYP, BYM, BY2, YCP, YCM, YC2) = range(25)
+NSEM = 25
 
 ORDER = (
-    ("VS", 0), ("VP", 0), ("M", 0, 0, 2), ("X", 0), ("M", 1, 0, 2), ("X", 1), ("SM", 0), ("SP", 0), ("M", 2, 0, 2),
-    ("SM", 1), ("SP", 1), ("M", 2, 2, 1), ("M", 3, 0, 2), ("X", 2), ("Y", 0), ("Y", 1), ("M", 4, 0, 2), ("X", 3),
-    ("SM", 2), ("SP", 2), ("H", 0), ("H", 1), ("SM", 3), ("SP", 3), ("B", 0), ("M", 4, 2, 1), ("B", 1),
-    ("M", 5, 0, 2), ("X", 4), ("Y", 2), ("CM", 0), ("CP", 0), ("CM", 1), ("CP", 1), ("Y", 3), ("M", 6, 0, 2),
-    ("X", 5), ("D", 0), ("SM", 4), ("SP", 4), ("H", 2), ("D", 1), ("H", 3), ("SM", 5), ("SP", 5), ("M", 7, 0, 2),
-    ("B", 2), ("M", 7, 2, 1), ("X", 6), ("B", 3), ("Y", 4), ("Y", 5), ("X", 7), ("CM", 2), ("CP", 2), ("SM", 6),
-    ("SP", 6), ("CM", 3), ("CP", 3), ("H", 4), ("D", 2), ("H", 5), ("SM", 7), ("SP", 7), ("D", 3), ("VT", 0),
-    ("B", 4), ("Y", 6), ("B", 5), ("E", 0), ("Y", 7), ("CM", 4), ("CP", 4), ("H", 6), ("CM", 5), ("CP", 5), ("E", 1),
-    ("D", 4), ("H", 7), ("B", 6), ("E", 2), ("D", 5), ("E", 3), ("B", 7), ("E", 4), ("CM", 6), ("CP", 6), ("E", 5),
-    ("CM", 7), ("CP", 7), ("D", 6), ("E", 6), ("D", 7), ("E", 7),
+    ("M", 0, 0, 2), ("X", 0), ("VS", 0), ("VP", 0), ("M", 1, 0, 2), ("X", 1), ("SP", 0), ("M", 2, 0, 2), ("SM", 0),
+    ("M", 2, 2, 1), ("SP", 1), ("SM", 1), ("X", 2), ("M", 3, 0, 2), ("M", 4, 0, 2), ("Y", 0), ("X", 3), ("Y", 1),
+    ("M", 5, 0, 2), ("SM", 2), ("SP", 2), ("H", 0), ("H", 1), ("SP", 3), ("SM", 3), ("X", 4), ("M", 5, 2, 1),
+    ("B", 0), ("M", 6, 0, 2), ("Y", 2), ("B", 1), ("Y", 3), ("X", 5), ("CM", 0), ("CP", 0), ("SM", 4), ("M", 6, 2, 1),
+    ("CM", 1), ("CP", 1), ("H", 2), ("H", 3), ("SM", 5), ("SP", 4), ("SP", 5), ("M", 7, 0, 2), ("D", 0), ("B", 2),
+    ("X", 6), ("Y", 4), ("B", 3), ("Y", 5), ("CM", 2), ("CP", 2), ("H", 4), ("SM", 6), ("SP", 6), ("CP", 3), ("D", 1),
+    ("CM", 3), ("X", 7), ("H", 5), ("B", 4), ("D", 2), ("VT", 0), ("Y", 6), ("SM", 7), ("SP", 7), ("D", 3), ("B", 5),
+    ("CM", 4), ("CP", 4), ("Y", 7), ("E", 0), ("H", 6), ("CM", 5), ("CP", 5), ("H", 7), ("D", 4), ("E", 1), ("CP", 6),
+    ("CM", 6), ("E", 2), ("E", 3), ("B", 7), ("D", 6), ("CM", 7), ("CP", 7), ("YM", 6), ("E", 4), ("D", 5), ("B", 6),
+    ("YP", 6), ("E", 5), ("Y2", 6), ("D", 7), ("E", 6), ("E", 7),
 )
 
 
 def kernel(
     ints, occ_t, virt, index, out,
-    ibuf, kron, expand, occ_rep, onehot, part, r1p, r1m, r2p, r2m, ry, gath, vraw, vblk, vrecv, vrows, vt, acc,
+    ibuf, kron, pick, onehot, part, r1p, r1m, r2p, r2m, ry, gath, vraw, vblk, vrecv, vrows, vt, acc,
     isem, vload, vsend, vrecv_sem, send, recv,
 ):
     row = lax.axis_index("row")
@@ -97,16 +99,16 @@
 
     for b in range(8):
         first = ((b % 2) * 4 + b // 2) * O_LOC
-        pick = jnp.where(iota((BLK, BLK), 1) == first + (iota((BLK, BLK), 0) >> 3), 1.0, 0.0).astype(BF)
-        occ_rep[b * BLK : (b + 1) * BLK, :] = jnp.dot(pick, occ_t[...], preferred_element_type=F32).astype(BF)
-    expand[...] = jnp.where(iota((N_MU, KROWS), 0) == (iota((N_MU, KROWS), 1) >> 3), 1.0, 0.0).astype(BF)
-
-    @pl.loop(0, 4)
-    def _(b):
-        rows = pl.ds(pl.multiple_of(b * (2 * BLK), 2 * BLK), 2 * BLK)
-        wide = jnp.dot(occ_rep[rows, :], expand[...], preferred_element_type=F32)
-        same = (iota((2 * BLK, KROWS), 0) & 7) == (iota((2 * BLK, KROWS), 1) & 7)
-        kron[rows, :] = jnp.where(same, wide, 0.0).astype(BF)
+        mine = iota((BLK, 8 * O_LOC), 1) == first + (iota((BLK, 8 * O_LOC), 0) >> 3)
+        pick[b * BLK : (b + 1) * BLK, :] = jnp.where(mine, 1.0, 0.0).astype(BF)
+    same = ((iota((8, NP), 0) & 7) == (iota((8, NP), 1) & 7))[None]
+    for j in range(0, N_MU, 32):
+        n = min(32, N_MU - j)
+        stretch = jnp.where(iota((n, 8 * n), 0) == (iota((n, 8 * n), 1) >> 3), 1.0, 0.0).astype(BF)
+        wide = jnp.dot(occ_t[:, j : j + n], stretch, preferred_element_type=F32).astype(BF)
+        wide = jnp.dot(pick[...], wide, preferred_element_type=F32).reshape(8 * O_LOC, 8, 8 * n)
+        wide = jnp.where(same[:, :, : 8 * n], wide, 0.0).astype(BF)
+        kron[:, 8 * j : 8 * (j + n)] = wide.reshape(8 * BLK, 8 * n)
 
     onehot[...] = jnp.where(iota((NP, NP), 0) == index[...], 1.0, 0.0).astype(BF)
 
@@ -238,8 +240,13 @@
     def whole(c, s, count=1):
         return gath.at[:, grows(c, s, count), :]
 
-    def half(c, s, lo):
-        return gath.at[pl.ds(lo, O_LOC // 2), grows(c, s, 2), :]
+    def pair(c, zz):
+        if c in Z_FIRST:
+            return grows(c, slot(zz, yl, core))
+        return grows(c, slot(zz, 0, core), 2)
+
+    def half(c, zz, lo):
+        return gath.at[pl.ds(lo, O_LOC // 2), pair(c, zz), :]
 
     def task_h(c):
         cps[c, YH].wait_recv()
@@ -261,33 +268,51 @@
     def task_b(c):
         cps[c, AY].wait_recv()
         g = whole(c, slot(z, 1 - yl, core))
-        go(c, BZP, g, g, d_zp)
-        go(c, BZM, g, g, d_zm)
+        if c not in Z_FIRST:
+            go(c, BZP, g, g, d_zp)
+            go(c, BZM, g, g, d_zm)
         go(c, BC, g, g, d_co)
+
+    def spread(c, zz, to_core, to_y):
+        g = gath.at[:, pair(c, zz), :]
+        go(c, to_core, g, g, d_co)
+        if c in Z_FIRST:
+            go(c, to_y, g, g, d_yl)
 
     def task_cp(c):
         cps[c, AZP].wait_recv()
-        cps[c, BZP].wait_recv()
-        s = slot(zm, 0, core)
-        g = half(c, s, 0)
+        if c not in Z_FIRST:
+            cps[c, BZP].wait_recv()
+        g = half(c, zm, 0)
         go(c, CZP, g, g, d_zp)
-        g = whole(c, s, 2)
-        go(c, CCP, g, g, d_co)
+        spread(c, zm, CCP, BYP)
 
     def task_cm(c):
         cps[c, AZM].wait_recv()
-        cps[c, BZM].wait_recv()
-        s = slot(zp, 0, core)
-        g = half(c, s, O_LOC // 2)
+        if c not in Z_FIRST:
+            cps[c, BZM].wait_recv()
+        g = half(c, zp, O_LOC // 2)
         go(c, CZM, g, g, d_zm)
-        g = whole(c, s, 2)
-        go(c, CCM, g, g, d_co)
+        spread(c, zp, CCM, BYM)
 
     def task_d(c):
         cps[c, CZP].wait_recv()
         cps[c, CZM].wait_recv()
-        g = whole(c, slot(z2, 0, core), 2)
-        go(c, DC, g, g, d_co)
+        spread(c, z2, DC, BY2)
+
+    def across(c, zz, arrived, to_core):
+        cps[c, arrived].wait_recv()
+        g = whole(c, slot(zz, 1 - yl, core))
+        go(c, to_core, g, g, d_co)
+
+    def task_yp(c):
+        across(c, zm, BYP, YCP)
+
+    def task_ym(c):
+        across(c, zp, BYM, YCM)
+
+    def task_y2(c):
+        across(c, z2, BY2, YC2)
 
     def task_vt(_):
         vlocal().wait()
@@ -310,13 +335,13 @@
             vt[:, pl.ds(o, 128)] = vrows[pl.ds(o, 128), :].astype(F32).T[:A_LOC].astype(BF)
 
     def task_e(c):
-        for k in (AC, BC, CCP, CCM, DC):
+        for k in (AC, BC, CCP, CCM, DC) + ((YCP, YCM, YC2) if c in Z_FIRST else ()):
             cps[c, k].wait_recv()
         ks = pl.ds(128 * STARTS[c], 128 * CHUNKS[c])
         lhs = vt[:, ks]
         last = c == len(CHUNKS) - 1
 
-        @pl.loop(0, O_LOC)
+        @pl.loop(0, O_LOC, unroll=O_LOC)
         def _(i):
             d = jnp.dot(lhs, gath[i, ks, :], preferred_element_type=F32)
             if c > 0:
@@ -327,7 +352,7 @@
                 acc[i] = d
 
     tasks = {"M": task_m, "X": task_x, "SP": task_sp, "SM": task_sm, "Y": task_y, "H": task_h, "B": task_b,
-             "CP": task_cp, "CM": task_cm, "D": task_d, "E": task_e, "VS": task_vs, "VP": task_vp, "VT": task_vt}
+             "YP": task_yp, "YM": task_ym, "Y2": task_y2, "CP": task_cp, "CM": task_cm, "D": task_d, "E": task_e, "VS": task_vs, "VP": task_vp, "VT": task_vt}
     for name, *where in ORDER:
         tasks[name](*where)
     for cp in sent:
@@ -346,8 +371,7 @@
         scratch_shapes=[
             pltpu.VMEM((NBUF, N_MU, 8, NP), BF),
             pltpu.VMEM((8 * BLK, KROWS), BF),
-            pltpu.VMEM((N_MU, KROWS), BF),
-            pltpu.VMEM((8 * BLK, N_MU), BF),
+            pltpu.VMEM((8 * BLK, 8 * O_LOC), BF),
             pltpu.VMEM((NP, NP), BF),
             pltpu.VMEM((TILES, 8 * BLK, NP), BF),
             pltpu.VMEM((TILES, BLK, NP), BF),

time: 109 us -> 103 us (0.945)
  Pallas kernels: 107 us -> 101 us
    pallas_call x1, Pallas kernels: 107 us -> 101 us  [local(): pl.pallas_call(kernel, out_shape=jax.ShapeDtypeStruct((O_LOC, A_LOC, NP),...]
where the time goes in v3:
time: 103 us
  Pallas kernels  101 us (98%)
  local copies, waits for them, and re-layouts  2.14 us (2%)
    pallas_call x1, Pallas kernels, local(): pl.pallas_call(kernel, out_shape=jax.ShapeDtypeStruct((O_LOC, A_LOC, NP),...  101 us
    unnamed x1, local copies, waits for them, and re-layouts  2.14 us

profile of v3, /device:TPU:1, one launch (start us, length us, event | category | flops | bytes accessed | tf_op | source)
XLA Modules:
  0.0 102.8 jit_solution(4014183646731704786)
XLA Ops:
  0.0 100.7 %shard_map.46 = bf16[12,144,256]{2,1,0:T(8,128)(2,1)} custom-call(bf16[300,150,256]{2,1,0:T(8,128)(2,1)} %ints.1, bf16[96,300]{1,0:T(8,128)(2,1)} %bitcast.2, bf16[150,2304]{1,0:T(8,128)(2,1)} %virt.1, s32[1,256]{1,0:T(1,128)} %bitcast.3), custom_call_target="tpu_custom_call" | custom-call | tf_op jit(solution)/shard_map/pallas_call | solution.py:366
  100.7 2.1 %copy.6 = bf16[12,144,256]{2,1,0:T(8,128)(2,1)} copy(bf16[12,144,256]{2,1,0:T(8,128)(2,1)} %shard_map.46) | data formatting | bytes 1769472

commit v4 on v3

--- a/solution.py
+++ b/solution.py
@@ -17,8 +17,8 @@
 A_LOC = 144
 NP = 256
 TILES = 19
-CHUNKS = (2, 2, 3, 2, 2, 3, 3, 2)
-Z_FIRST = (6,)
+CHUNKS = (2, 1, 3, 4, 2, 2, 3, 2)
+Z_FIRST = (1, 4, 7)
 STARTS = tuple(sum(CHUNKS[:k]) for k in range(len(CHUNKS)))
 BLK = O_LOC * 8
 KROWS = N_MU * 8
@@ -28,17 +28,32 @@
  BYP, BYM, BY2, YCP, YCM, YC2) = range(25)
 NSEM = 25
 
-ORDER = (
-    ("M", 0, 0, 2), ("X", 0), ("VS", 0), ("VP", 0), ("M", 1, 0, 2), ("X", 1), ("SP", 0), ("M", 2, 0, 2), ("SM", 0),
-    ("M", 2, 2, 1), ("SP", 1), ("SM", 1), ("X", 2), ("M", 3, 0, 2), ("M", 4, 0, 2), ("Y", 0), ("X", 3), ("Y", 1),
-    ("M", 5, 0, 2), ("SM", 2), ("SP", 2), ("H", 0), ("H", 1), ("SP", 3), ("SM", 3), ("X", 4), ("M", 5, 2, 1),
-    ("B", 0), ("M", 6, 0, 2), ("Y", 2), ("B", 1), ("Y", 3), ("X", 5), ("CM", 0), ("CP", 0), ("SM", 4), ("M", 6, 2, 1),
-    ("CM", 1), ("CP", 1), ("H", 2), ("H", 3), ("SM", 5), ("SP", 4), ("SP", 5), ("M", 7, 0, 2), ("D", 0), ("B", 2),
-    ("X", 6), ("Y", 4), ("B", 3), ("Y", 5), ("CM", 2), ("CP", 2), ("H", 4), ("SM", 6), ("SP", 6), ("CP", 3), ("D", 1),
-    ("CM", 3), ("X", 7), ("H", 5), ("B", 4), ("D", 2), ("VT", 0), ("Y", 6), ("SM", 7), ("SP", 7), ("D", 3), ("B", 5),
-    ("CM", 4), ("CP", 4), ("Y", 7), ("E", 0), ("H", 6), ("CM", 5), ("CP", 5), ("H", 7), ("D", 4), ("E", 1), ("CP", 6),
-    ("CM", 6), ("E", 2), ("E", 3), ("B", 7), ("D", 6), ("CM", 7), ("CP", 7), ("YM", 6), ("E", 4), ("D", 5), ("B", 6),
-    ("YP", 6), ("E", 5), ("Y2", 6), ("D", 7), ("E", 6), ("E", 7),
+STEPS = (
+    (),
+    (("X", 0), ("VS", 0),),
+    (("VP", 0), ("X", 1),),
+    (("SP", 0), ("SM", 0),),
+    (),
+    (("X", 2),),
+    (("SM", 1),),
+    (),
+    (("Y", 0),),
+    (("SP", 1),),
+    (("SM", 2), ("SP", 2),),
+    (),
+    (("Y", 1), ("X", 3),),
+    (),
+    (("Y", 2),),
+    (("H", 1),),
+    (("H", 0), ("SP", 3), ("SM", 3), ("H", 2), ("CM", 1), ("CP", 1), ("VT", 0), ("X", 4), ("X", 5), ("B", 0),
+     ("Y", 3), ("B", 2),),
+    (("CM", 0), ("SP", 4), ("CP", 0), ("D", 1), ("SM", 4),),
+    (("YP", 1), ("SP", 5), ("B", 1), ("SM", 5), ("CM", 2), ("CP", 2), ("H", 3), ("Y2", 1), ("X", 6), ("D", 0),
+     ("Y", 4), ("E", 0), ("Y", 5), ("YM", 1), ("D", 2), ("B", 3), ("SP", 6), ("SM", 6), ("E", 1), ("X", 7),
+     ("H", 4), ("H", 5), ("CP", 3), ("CM", 3), ("Y", 6), ("SP", 7), ("SM", 7), ("B", 5), ("CP", 4), ("CM", 4),
+     ("Y", 7), ("H", 6), ("D", 3), ("B", 4), ("E", 2), ("CP", 5), ("YM", 4), ("E", 3), ("YP", 4), ("CM", 5),
+     ("D", 4), ("H", 7), ("B", 6), ("CM", 7), ("Y2", 4), ("CP", 7), ("CP", 6), ("CM", 6), ("D", 5), ("E", 4),
+     ("D", 7), ("E", 5), ("YP", 7), ("YM", 7), ("D", 6), ("Y2", 7), ("B", 7), ("E", 6), ("E", 7),),
 )
 
 
@@ -117,19 +132,28 @@
     sent = []
 
     def remote(src, dst, c, k, dev):
-        cp = pltpu.make_async_remote_copy(
+        return pltpu.make_async_remote_copy(
             src_ref=src, dst_ref=dst, send_sem=send.at[c * NSEM + k], recv_sem=recv.at[c * NSEM + k],
             device_id=dev, device_id_type=MESH,
         )
-        return cp
-
-    cps = {}
 
     def go(c, k, src, dst, dev):
-        cp = remote(src, dst, c, k, dev)
-        cp.start()
-        cps[c, k] = cp
-        sent.append(cp)
+        remote(src, dst, c, k, dev).start()
+        sent.append((c, k))
+
+    def like(c, k):
+        n = CHUNKS[c]
+        rows = 8 * n * (2 if k in (CZP, CZM, CCP, CCM, DC) and c not in Z_FIRST else 1)
+        if k <= YH:
+            ref = part.at[pl.ds(0, n), pl.ds(0, BLK), :]
+        elif k in (CZP, CZM):
+            ref = gath.at[pl.ds(0, O_LOC // 2), pl.ds(0, rows), :]
+        else:
+            ref = gath.at[:, pl.ds(0, rows), :]
+        return remote(ref, ref, c, k, d_co)
+
+    def arrived(c, k):
+        like(c, k).wait_recv()
 
     def vcopy(k):
         to = (col + k) % 16
@@ -162,29 +186,27 @@
     def blk(xx, yy):
         return pl.ds(pl.multiple_of(xx * (2 * BLK) + yy * BLK, BLK), BLK)
 
-    def task_m(c, first, count):
-        @pl.loop(STARTS[c] + first, STARTS[c] + first + count)
-        def _(t):
-            s = t % NBUF
-
-            @pl.when(t < TILES - 1)
-            def _():
-                icopy(t, s).wait()
-
-            @pl.when(t == TILES - 1)
-            def _():
-                icopy_last(s).wait()
-
-            rhs = ibuf[s].reshape(KROWS, NP)
-            part[t] = jnp.dot(kron[...], rhs, preferred_element_type=F32).astype(BF)
-
-            @pl.when(t + NBUF < TILES - 1)
-            def _():
-                icopy(t + NBUF, s).start()
-
-            @pl.when(t + NBUF == TILES - 1)
-            def _():
-                icopy_last(s).start()
+    def product(t):
+        s = t % NBUF
+
+        @pl.when(t < TILES - 1)
+        def _():
+            icopy(t, s).wait()
+
+        @pl.when(t == TILES - 1)
+        def _():
+            icopy_last(s).wait()
+
+        rhs = ibuf[s].reshape(KROWS, NP)
+        part[t] = jnp.dot(kron[...], rhs, preferred_element_type=F32).astype(BF)
+
+        @pl.when(t + NBUF < TILES - 1)
+        def _():
+            icopy(t + NBUF, s).start()
+
+        @pl.when(t + NBUF == TILES - 1)
+        def _():
+            icopy_last(s).start()
 
     def task_x(c):
         ts = tiles(c)
@@ -198,7 +220,7 @@
 
     def task_sp(c):
         ts = tiles(c)
-        cps[c, X1P].wait_recv()
+        arrived(c, X1P)
 
         @functools.partial(each_tile, c)
         def _(t):
@@ -209,7 +231,7 @@
 
     def task_sm(c):
         ts = tiles(c)
-        cps[c, X1M].wait_recv()
+        arrived(c, X1M)
 
         @functools.partial(each_tile, c)
         def _(t):
@@ -225,7 +247,7 @@
     def task_y(c):
         ts = tiles(c)
         for k in (RAWP, RAWM, ACCP, ACCM):
-            cps[c, k].wait_recv()
+            arrived(c, k)
 
         @functools.partial(each_tile, c)
         def _(t):
@@ -249,7 +271,7 @@
         return gath.at[pl.ds(lo, O_LOC // 2), pair(c, zz), :]
 
     def task_h(c):
-        cps[c, YH].wait_recv()
+        arrived(c, YH)
         base = 128 * STARTS[c] + me * (8 * CHUNKS[c])
 
         @functools.partial(each_tile, c)
@@ -266,7 +288,7 @@
         go(c, AC, g, g, d_co)
 
     def task_b(c):
-        cps[c, AY].wait_recv()
+        arrived(c, AY)
         g = whole(c, slot(z, 1 - yl, core))
         if c not in Z_FIRST:
             go(c, BZP, g, g, d_zp)
@@ -280,28 +302,28 @@
             go(c, to_y, g, g, d_yl)
 
     def task_cp(c):
-        cps[c, AZP].wait_recv()
+        arrived(c, AZP)
         if c not in Z_FIRST:
-            cps[c, BZP].wait_recv()
+            arrived(c, BZP)
         g = half(c, zm, 0)
         go(c, CZP, g, g, d_zp)
         spread(c, zm, CCP, BYP)
 
     def task_cm(c):
-        cps[c, AZM].wait_recv()
+        arrived(c, AZM)
         if c not in Z_FIRST:
-            cps[c, BZM].wait_recv()
+            arrived(c, BZM)
         g = half(c, zp, O_LOC // 2)
         go(c, CZM, g, g, d_zm)
         spread(c, zp, CCM, BYM)
 
     def task_d(c):
-        cps[c, CZP].wait_recv()
-        cps[c, CZM].wait_recv()
+        arrived(c, CZP)
+        arrived(c, CZM)
         spread(c, z2, DC, BY2)
 
-    def across(c, zz, arrived, to_core):
-        cps[c, arrived].wait_recv()
+    def across(c, zz, landed, to_core):
+        arrived(c, landed)
         g = whole(c, slot(zz, 1 - yl, core))
         go(c, to_core, g, g, d_co)
 
@@ -336,7 +358,7 @@
 
     def task_e(c):
         for k in (AC, BC, CCP, CCM, DC) + ((YCP, YCM, YC2) if c in Z_FIRST else ()):
-            cps[c, k].wait_recv()
+            arrived(c, k)
         ks = pl.ds(128 * STARTS[c], 128 * CHUNKS[c])
         lhs = vt[:, ks]
         last = c == len(CHUNKS) - 1
@@ -351,12 +373,24 @@
             else:
                 acc[i] = d
 
-    tasks = {"M": task_m, "X": task_x, "SP": task_sp, "SM": task_sm, "Y": task_y, "H": task_h, "B": task_b,
-             "YP": task_yp, "YM": task_ym, "Y2": task_y2, "CP": task_cp, "CM": task_cm, "D": task_d, "E": task_e, "VS": task_vs, "VP": task_vp, "VT": task_vt}
-    for name, *where in ORDER:
-        tasks[name](*where)
-    for cp in sent:
-        cp.wait_send()
+    tasks = {"X": task_x, "SP": task_sp, "SM": task_sm, "Y": task_y, "H": task_h, "B": task_b,
+             "CP": task_cp, "CM": task_cm, "D": task_d, "YP": task_yp, "YM": task_ym, "Y2": task_y2,
+             "E": task_e, "VS": task_vs, "VP": task_vp, "VT": task_vt}
+
+    def steps(k):
+        for name, c in STEPS[k]:
+            tasks[name](c)
+
+    @pl.loop(0, TILES)
+    def _(t):
+        product(t)
+        for k in range(TILES - 1):
+            if STEPS[k]:
+                pl.when(t == k)(functools.partial(steps, k))
+
+    steps(TILES - 1)
+    for c, k in sent:
+        like(c, k).wait_send()
 
 
 def local(integrals, occ_coef, virt_coef, pair_index):
@@ -365,7 +399,7 @@
     hbm = pl.BlockSpec(memory_space=pl.ANY)
     return pl.pallas_call(
         kernel,
-        out_shape=jax.ShapeDtypeStruct((O_LOC, A_LOC, NP), BF),
+        out_shape=pltpu.VMEM((O_LOC, A_LOC, NP), BF),
         in_specs=[hbm, vm, hbm, vm],
         out_specs=vm,
         scratch_shapes=[

time: 103 us -> 100 us (0.971)
  Pallas kernels: 101 us -> 99.3 us
  local copies, waits for them, and re-layouts: 2.14 us -> 0.91 us
    pallas_call x1, Pallas kernels: 101 us -> 99.3 us  [local(): pl.pallas_call(kernel, out_shape=pltpu.VMEM((O_LOC, A_LOC, NP), BF), in_s...]
    unnamed x1, local copies, waits for them, and re-layouts: 2.14 us -> 0.91 us
where the time goes in v4:
time: 100 us
  Pallas kernels  99.3 us (99%)
    pallas_call x1, Pallas kernels, local(): pl.pallas_call(kernel, out_shape=pltpu.VMEM((O_LOC, A_LOC, NP), BF), in_s...  99.3 us

profile of v4, /device:TPU:1, one launch (start us, length us, event | category | flops | bytes accessed | tf_op | source)
XLA Modules:
  0.0 100.3 jit_solution(15958328386543201697)
XLA Ops:
  0.0 99.3 %shard_map.46 = bf16[12,144,256]{2,1,0:T(8,128)(2,1)S(1)} custom-call(bf16[300,150,256]{2,1,0:T(8,128)(2,1)} %ints.1, bf16[96,300]{1,0:T(8,128)(2,1)} %bitcast.2, bf16[150,2304]{1,0:T(8,128)(2,1)} %virt.1, s32[1,256]{1,0:T(1,128)} %bitcast.3), custom_call_target="tpu_custom_call" | custom-call | tf_op jit(solution)/shard_map/pallas_call | solution.py:400
  99.3 0.9 copy.6
